TPU v7x, 32 devices: a whole 2x2x4 slice. The times are simulated.
32 devices in a mesh: row: 8 (over z, x), col: 4 (over y, core).
Axes of the slice: x: 2, y: 2, z: 4, core: 2. Of those that a mesh axis runs over, the one named last changes fastest.
Arguments:
- snapshot: bfloat16 [512, 256, 512], P('row', 'col'), may hold values from -6 to 6
- basis_two: bfloat16 [256, 128], P('col'), may hold values from -0.375 to 0.375
- basis_three: bfloat16 [512, 128], replicated, may hold values from -0.25 to 0.25
Outputs:
- gram: float32 [512, 512], P('row', 'col')
All inputs are finite; a program needn't handle non-finite values.
Results may differ from a plain program's by a relative error of at most 0.0017.
Values may be sent and summed in bfloat16 or wider, within the bound.
No kernel may reach another device: no remote copies, remote signals or barrier semaphores. Data moves between devices by JAX's collectives and lax.ppermute only.
A program may use at most 64 MiB of HBM per device.

v0:
```python
import jax
import jax.numpy as jnp
from jax import lax
from jax.sharding import PartitionSpec as P


def on_device(snapshot, basis_two, basis_three):
    cells_one, cells_two, cells_three = snapshot.shape
    ranks_two = basis_two.shape[1]
    ranks_three = basis_three.shape[1]
    inner = jnp.dot(
        snapshot.reshape(cells_one * cells_two, cells_three),
        basis_three,
        preferred_element_type=jnp.float32,
    )
    inner = inner.astype(jnp.bfloat16).reshape(cells_one, cells_two, ranks_three)
    regrouped = lax.all_to_all(inner, "col", split_axis=2, concat_axis=1, tiled=True)
    whole_factor = lax.all_gather(basis_two, "col", axis=0, tiled=True)
    full = jnp.einsum("abr,bq->qar", regrouped, whole_factor, preferred_element_type=jnp.float32)
    rounded = lax.all_to_all(
        full.astype(jnp.bfloat16), "col", split_axis=0, concat_axis=2, tiled=True
    )
    partial_gram = jnp.einsum(
        "qar,qbr->ab",
        rounded,
        lax.all_gather(rounded, "row", axis=1, tiled=True),
        preferred_element_type=jnp.float32,
    )
    summed_gram = lax.psum_scatter(partial_gram, "col", scatter_dimension=1, tiled=True)
    return summed_gram * (1.0 / (ranks_two * ranks_three))


def solution(mesh):
    in_specs = (P("row", "col", None), P("col", None), P())
    out_specs = P("row", "col")
    return jax.shard_map(
        on_device, mesh=mesh, in_specs=in_specs, out_specs=out_specs, check_vma=False
    )
```

profile of v0, /device:TPU:0, one launch (start us, length us, event | category | flops | bytes accessed | tf_op | source)
XLA Modules:
  0.0 165.3 jit_solution(16451007527104671222)
XLA Ops:
  6.5 0.0 copy-start
  6.5 0.9 copy-done
  7.4 3.4 %convolution_convert_fusion = bf16[4096,128]{1,0:T(8,128)(2,1)S(1)} fusion(bf16[4096,512]{1,0:T(8,128)(2,1)} %bitcast.31, bf16[512,128]{1,0:T(8,128)(2,1)S(1)} %copy-done), kind=kOutput, calls=%fused_computation | convolution fusion | flops 537395200 | bytes 5373952 | tf_op jit(solution)/shard_map/dot_general | solution.py:11
  10.9 0.0 copy-start.1
  10.9 3.0 %copy.20 = bf16[64,64,128]{1,0,2:T(8,128)(2,1)S(1)} copy(bf16[64,64,128]{2,1,0:T(8,128)(2,1)S(1)} %bitcast.32) | data formatting | bytes 2097152 | tf_op jit(solution)/shard_map/reshape | solution.py:16
  13.9 2.6 %reshape.10 = bf16[4,2,65536]{2,1,0:T(2,128)(2,1)} reshape(bf16[128,64,64]{2,1,0:T(8,128)(2,1)S(1)} %bitcast.29) | data formatting | bytes 2097152
  16.5 4.3 %all-to-all-start = ((bf16[4,2,65536]{2,1,0:T(2,128)(2,1)}), bf16[4,2,65536]{2,1,0:T(2,128)(2,1)S(1)}, u32[]{:S(2)}, u32[]{:S(2)}) async-start(bf16[4,2,65536]{2,1,0:T(2,128)(2,1)} %reshape.10), calls=%async_computation | async-start | bytes 2097152 | tf_op jit(solution)/shard_map/all_to_all | solution.py:17
  20.8 0.0 all-gather.2.cloned.1.call-start
  20.8 0.0 copy-done.1
  20.8 15.6 %all_gather.6 = bf16[256,128]{1,0:T(8,128)(2,1)S(1)} all-gather(bf16[64,128]{1,0:T(8,128)(2,1)S(1)} %copy-done.1), channel_id=1, replica_groups=mesh['row'=8,'col'=4] {'col'}, dimensions={0}, use_global_device_ids=true | all-gather | bytes 81920 | tf_op jit(solution)/shard_map/all_gather | solution.py:18
  36.4 0.0 all-to-all-done
  36.4 1.4 reshape.11
  37.8 3.0 %copy.22 = bf16[64,4,64,32]{2,1,3,0:T(4,128)(2,1)} copy(bf16[64,4,64,32]{2,0,3,1:T(8,128)(2,1)S(1)} %bitcast.30) | data formatting | bytes 2097152 | tf_op jit(solution)/shard_map/all_to_all | solution.py:17
  40.8 3.5 %all_to_all.29 = bf16[64,256,32]{1,2,0:T(8,128)(2,1)S(1)} reshape(bf16[64,4,64,32]{2,1,3,0:T(4,128)(2,1)} %copy.22) | data formatting | bytes 2097152 | tf_op jit(solution)/shard_map/all_to_all | solution.py:17
  44.3 0.4 fusion
  44.7 1.7 %copy.23 = bf16[128,64,32]{1,2,0:T(8,128)(2,1)S(1)} copy(bf16[128,64,32]{0,2,1:T(8,128)(2,1)S(1)} %fusion) | data formatting | bytes 1048576 | tf_op jit(solution)/shard_map/convert_element_type | solution.py:21
  46.4 0.9 reshape.12
  47.3 11.2 %all_to_all.36 = bf16[4,2,32768]{2,1,0:T(2,128)(2,1)S(1)} all-to-all(bf16[4,2,32768]{2,1,0:T(2,128)(2,1)S(1)} %reshape.12), channel_id=1, replica_groups=mesh['row'=8,'col'=4] {'col'}, dimensions={0} | all-to-all | bytes 1048576 | tf_op jit(solution)/shard_map/all_to_all | solution.py:20
  58.5 0.7 reshape.13
  59.2 0.1 copy.24
  59.4 1.1 copy.25
  60.5 0.0 all-gather.2.cloned.1.call-update
  60.5 0.0 reduce-scatter.2.cloned.1.call-start
  60.6 73.9 %all-gather.2.cloned.1.call-done = bf16[32,512,128]{2,1,0:T(8,128)(2,1)} async-done(((bf16[32,64,128]{2,1,0:T(8,128)(2,1)}), bf16[32,512,128]{2,1,0:T(8,128)(2,1)}) %all-gather.2.cloned.1.call-update) | async-done | bytes 4194320 | tf_op jit(solution)/shard_map/all_gather | solution.py:26
  134.4 4.2 %convolution_bitcast_fusion = f32[64,512]{1,0:T(8,128)} fusion(bf16[32,64,128]{1,2,0:T(8,128)(2,1)S(1)} %bitcast.28, bf16[32,512,128]{2,1,0:T(8,128)(2,1)} %all-gather.2.cloned.1.call-done), kind=kOutput, calls=%fused_computation.3 | convolution fusion | flops 268435456 | bytes 4849664 | tf_op jit(solution)/shard_map/qar,qbr->ab/dot_general | solution.py:23
  138.7 0.0 reduce-scatter.2.cloned.1.call-update
  138.7 18.3 %reduce-scatter.2.cloned.1.call-done = f32[64,128]{1,0:T(8,128)} async-done(((f32[64,512]{1,0:T(8,128)}), f32[64,128]{1,0:T(8,128)}) %reduce-scatter.2.cloned.1.call-update) | async-done | bytes 32784 | tf_op jit(solution)/shard_map/reduce_scatter | solution.py:29
  157.0 1.4 broadcast_multiply_fusion
Async XLA Ops:
  6.5 0.9 copy-start
  10.9 9.9 %copy-start.1 = (bf16[64,128]{1,0:T(8,128)(2,1)S(1)}, bf16[64,128]{1,0:T(8,128)(2,1)}, u32[]{:S(2)}) copy-start(bf16[64,128]{1,0:T(8,128)(2,1)} %param.4) | copy-start | bytes 49156
  16.5 19.9 %all-to-all-start = ((bf16[4,2,65536]{2,1,0:T(2,128)(2,1)}), bf16[4,2,65536]{2,1,0:T(2,128)(2,1)S(1)}, u32[]{:S(2)}, u32[]{:S(2)}) async-start(bf16[4,2,65536]{2,1,0:T(2,128)(2,1)} %reshape.10), calls=%async_computation | async-start | bytes 2097152 | tf_op jit(solution)/shard_map/all_to_all | solution.py:17
  20.8 113.7 %all-gather.2.cloned.1.call-start = ((), (), s32[]{:S(2)}) async-start(), calls=%async_computation.3 | async-start | bytes 4718592 | tf_op jit(solution)/shard_map/all_gather | solution.py:26
  60.5 96.5 %reduce-scatter.2.cloned.1.call-start = ((), (), s32[]{:S(2)}) async-start(), calls=%async_computation.4 | async-start | bytes 163840 | tf_op jit(solution)/shard_map/reduce_scatter | solution.py:29
Sparse Core Ops, SparseCore 0:
  60.6 73.7 all-gather.1
  138.8 18.1 reduce-scatter.1
where the time goes:
time: 166 us; the launch traced here: 165 us
  waiting for transfers between devices  92.3 us (56%)
  blocking collectives  26.8 us (16%)
  local copies, waits for them, and re-layouts  18.9 us (11%)
  between operations  13.5 us (8%)
  matrix products  8.09 us (5%)
  starting transfers between devices  4.3 us (3%)
    all_gather x1, waiting for transfers between devices, on_device(): lax.all_gather(rounded, 'row', axis=1, tiled=True)  73.9 us
    reduce_scatter x1, waiting for transfers between devices, on_device(): lax.psum_scatter(partial_gram, 'col', scatter_dimension=1, tiled=True)  18.3 us
    all_gather x1, blocking collectives, on_device(): whole_factor = lax.all_gather(basis_two, 'col', axis=0, tiled=True)  15.6 us
    all_to_all x1, blocking collectives, on_device(): lax.all_to_all(full.astype(jnp.bfloat16), 'col', split_axis=0, concat_axi...  11.2 us
    unnamed x8, local copies, waits for them, and re-layouts  6.55 us
    all_to_all x2, local copies, waits for them, and re-layouts, on_device(): lax.all_to_all(inner, 'col', split_axis=2, concat_axis=1, tiled=True)  6.45 us
    all_to_all x1, starting transfers between devices, on_device(): lax.all_to_all(inner, 'col', split_axis=2, concat_axis=1, tiled=True)  4.26 us
    dot_general x1, matrix products, on_device(): jnp.einsum('qar,qbr->ab', rounded, lax.all_gather(rounded, 'row', axis=1,...  4.22 us
  transfers between devices with their start and end apart: 3, of which 2 were waited for; matrix products, arithmetic and copies ran while one was open for 0% of the time, Pallas kernels for 0%

commit v1 on v0

v1 whole, which is shorter than its diff:
```python
import functools

import jax
import jax.numpy as jnp
from jax import lax
from jax.experimental import pallas as pl
from jax.experimental.pallas import tpu as pltpu
from jax.sharding import PartitionSpec as P

VMEM = pltpu.VMEM
MIB = 1024 * 1024


def swap_blocks(tiles, width):
    count = len(tiles)
    lane = lax.broadcasted_iota(jnp.int32, tiles[0].shape, 1) // width
    outs = []
    for j in range(count):
        out = None
        for g in range(count):
            shift = ((g - j) * width) % (count * width)
            moved = tiles[g] if shift == 0 else pltpu.roll(tiles[g], shift, 1)
            out = moved if out is None else jnp.where(lane == g, moved, out)
        outs.append(out)
    return outs


def project_three_kernel(chunks, snap, three, two, out, buf, three_buf, two_buf, sems):
    groups, steps, cells_two, cells_three = snap.shape
    per = steps // chunks
    width = three.shape[1] // groups
    copies = [
        pltpu.make_async_copy(three, three_buf, sems.at[chunks]),
        pltpu.make_async_copy(two, two_buf, sems.at[chunks + 1]),
    ]
    for n in range(chunks):
        part = (slice(None), pl.ds(n * per, per))
        copies.append(pltpu.make_async_copy(snap.at[part], buf.at[part], sems.at[n]))
    for copy in copies:
        copy.start()
    copies[0].wait()
    weights = three_buf[...]
    for n in range(chunks):
        copies[2 + n].wait()
        rows = per * cells_two
        inner = [
            jnp.dot(
                buf[g, n * per : (n + 1) * per].reshape(rows, cells_three),
                weights,
                preferred_element_type=jnp.float32,
            )
            for g in range(groups)
        ]
        for j, piece in enumerate(swap_blocks(inner, width)):
            out[j, n * rows : (n + 1) * rows, :] = piece.astype(jnp.bfloat16)
    copies[1].wait()
    for j in range(groups):
        out[j, steps * cells_two :, :] = two_buf[...]


def project_three(snapshot, basis_two, basis_three, cols):
    cells_one, cells_two, cells_three = snapshot.shape
    ranks_two = basis_two.shape[1]
    ranks_three = basis_three.shape[1]
    steps = cells_one // cols
    snap = snapshot.reshape(cols, steps, cells_two, cells_three)
    if ranks_two != 128 or ranks_three != 128 or steps % 16 or ranks_three // cols < 32:
        inner = jnp.einsum(
            "gtbc,cr->gtbr", snap, basis_three, preferred_element_type=jnp.float32
        ).astype(jnp.bfloat16)
        inner = inner.reshape(cols, steps, cells_two, cols, ranks_three // cols)
        inner = inner.transpose(3, 1, 2, 0, 4)
        inner = inner.reshape(cols, steps * cells_two, ranks_three)
        two = jnp.broadcast_to(basis_two, (cols,) + basis_two.shape)
        return jnp.concatenate([inner, two], axis=1)
    chunks = 4
    rows = (steps + 1) * cells_two
    return pl.pallas_call(
        functools.partial(project_three_kernel, chunks),
        out_shape=jax.ShapeDtypeStruct((cols, rows, ranks_three), jnp.bfloat16),
        in_specs=[pl.BlockSpec(memory_space=pltpu.HBM)] * 3,
        out_specs=pl.BlockSpec(memory_space=VMEM),
        scratch_shapes=[
            VMEM(snap.shape, jnp.bfloat16),
            VMEM(basis_three.shape, jnp.bfloat16),
            VMEM(basis_two.shape, jnp.bfloat16),
            pltpu.SemaphoreType.DMA((chunks + 2,)),
        ],
        compiler_params=pltpu.CompilerParams(vmem_limit_bytes=20 * MIB),
        name="project_three",
    )(snap, basis_three, basis_two)


def project_two_kernel(recv, out, held):
    cols, rows, width = recv.shape
    dests, part, _ = out.shape
    ranks_two = held.shape[0] // (dests * part // recv.shape[2])
    ranks_two = recv.shape[2]
    steps = dests * part // ranks_two
    cells = rows // (steps + 1)
    factor = jnp.concatenate([recv[j, steps * cells :, :] for j in range(cols)], axis=0)
    factor = factor.astype(jnp.float32).T.astype(jnp.bfloat16)
    for t in range(steps):
        inner = jnp.concatenate(
            [recv[j, t * cells : (t + 1) * cells, :] for j in range(cols)], axis=0
        )
        held[pl.ds(t, ranks_two, stride=steps), :] = jnp.dot(
            factor, inner, preferred_element_type=jnp.float32
        )
    out[...] = held[...].astype(jnp.bfloat16).reshape(out.shape)


def project_two(recv, rows, cells_two):
    cols, height, width = recv.shape
    steps = height // cells_two - 1
    ranks_two = width
    shape = (rows, steps * ranks_two // rows, width)
    if steps % 16 or width != 128 or ranks_two % rows:
        inner = recv[:, : steps * cells_two].reshape(cols, steps, cells_two, width)
        factor = recv[:, steps * cells_two :]
        full = jnp.einsum("jtbl,jbq->qtl", inner, factor, preferred_element_type=jnp.float32)
        return full.astype(jnp.bfloat16).reshape(shape)
    return pl.pallas_call(
        project_two_kernel,
        out_shape=jax.ShapeDtypeStruct(shape, jnp.bfloat16),
        in_specs=[pl.BlockSpec(memory_space=VMEM)],
        out_specs=pl.BlockSpec(memory_space=VMEM),
        scratch_shapes=[VMEM((steps * ranks_two, width), jnp.float32)],
        compiler_params=pltpu.CompilerParams(vmem_limit_bytes=20 * MIB),
        name="project_two",
    )(recv)


def gram_kernel(cols, recv, out, held):
    rows, part, width = recv.shape
    dests, cells_one, cells_out = out.shape
    steps = cells_one // cols
    ranks = part // steps
    block = width // cols
    for i in range(rows):
        for u in range(ranks // cols):
            tiles = [
                recv[i, (u * cols + p) * steps : (u * cols + p + 1) * steps, :].astype(
                    jnp.float32
                )
                for p in range(cols)
            ]
            for g, tile in enumerate(swap_blocks(tiles, block)):
                base = i * cells_one + g * steps
                held[base : base + steps, u * width : (u + 1) * width] = tile.astype(
                    jnp.bfloat16
                )
    right = held[...]
    for i in range(rows):
        left = held[i * cells_one : (i + 1) * cells_one, :]
        gram = lax.dot_general(
            left, right, (((1,), (1,)), ((), ())), preferred_element_type=jnp.float32
        ).astype(out.dtype)
        for j in range(cols):
            out[i * cols + j] = gram[:, j * cells_out : (j + 1) * cells_out]


def partial_gram(recv, cells_one, cols):
    rows, part, width = recv.shape
    steps = cells_one // cols
    ranks = part // steps
    block = width // cols
    cells_out = rows * cells_one // cols
    shape = (rows * cols, cells_one, cells_out)
    if steps % 16 or width != 128 or ranks % cols or cells_out % 128:
        flat = recv.reshape(rows, ranks, steps, cols, block).transpose(0, 3, 2, 1, 4)
        flat = flat.reshape(rows * cells_one, ranks * block)
        gram = jnp.einsum("ak,ek->ae", flat, flat, preferred_element_type=jnp.float32)
        gram = gram.reshape(rows, cells_one, cols, cells_out).transpose(0, 2, 1, 3)
        return gram.reshape(shape).astype(jnp.bfloat16)
    return pl.pallas_call(
        functools.partial(gram_kernel, cols),
        out_shape=jax.ShapeDtypeStruct(shape, jnp.bfloat16),
        in_specs=[pl.BlockSpec(memory_space=VMEM)],
        out_specs=pl.BlockSpec(memory_space=VMEM),
        scratch_shapes=[VMEM((rows * cells_one, ranks * block), jnp.bfloat16)],
        compiler_params=pltpu.CompilerParams(vmem_limit_bytes=20 * MIB),
        name="partial_gram",
    )(recv)


def on_device(rows, cols, snapshot, basis_two, basis_three):
    cells_one, cells_two, _ = snapshot.shape
    ranks_two = basis_two.shape[1]
    ranks_three = basis_three.shape[1]
    pieces = project_three(snapshot, basis_two, basis_three, cols)
    pieces = lax.all_to_all(pieces, "col", split_axis=0, concat_axis=0, tiled=True)
    shares = project_two(pieces, rows, cells_two)
    shares = lax.all_to_all(shares, "row", split_axis=0, concat_axis=0, tiled=True)
    parts = partial_gram(shares, cells_one, cols)
    parts = lax.all_to_all(parts, ("row", "col"), split_axis=0, concat_axis=0, tiled=True)
    total = jnp.sum(parts.astype(jnp.float32), axis=0)
    return total * (1.0 / (ranks_two * ranks_three))


def solution(mesh):
    in_specs = (P("row", "col", None), P("col", None), P())
    return jax.shard_map(
        functools.partial(on_device, mesh.shape["row"], mesh.shape["col"]),
        mesh=mesh,
        in_specs=in_specs,
        out_specs=P("row", "col"),
        check_vma=False,
    )
```

time: 166 us -> 67.2 us (0.40)
  waiting for transfers between devices: 92.3 us -> 0 us
  blocking collectives: 26.8 us -> 57.4 us
  local copies, waits for them, and re-layouts: 18.9 us -> 3.81 us
  between operations: 13.5 us -> 0.03 us
  matrix products: 8.09 us -> 0 us
  Pallas kernels: 0 us -> 4.96 us
  starting transfers between devices: 4.3 us -> 0 us
    all_gather x1 -> x0, waiting for transfers between devices: 73.9 us -> none  [on_device(): lax.all_gather(rounded, 'row', axis=1, tiled=True)]
    all_to_all x1 -> x3, blocking collectives: 11.2 us -> 57.4 us  [the longest x1 20.1 us: on_device(): lax.all_to_all(shares, 'row', split_axis=0, concat_axis=0, tiled=True)]
    reduce_scatter x1 -> x0, waiting for transfers between devices: 18.3 us -> none  [on_device(): lax.psum_scatter(partial_gram, 'col', scatter_dimension=1, tiled=True)]
    all_gather x1 -> x0, blocking collectives: 15.6 us -> none  [on_device(): whole_factor = lax.all_gather(basis_two, 'col', axis=0, tiled=True)]
    dot_general x3 -> x0, matrix products: 8.09 us -> none  [the longest x1 4.22 us: on_device(): jnp.einsum('qar,qbr->ab', rounded, lax.all_gather(rounded, 'row', axis=1,...]
    all_to_all x4 -> x0, local copies, waits for them, and re-layouts: 7.72 us -> none  [the longest x2 6.45 us: on_device(): lax.all_to_all(inner, 'col', split_axis=2, concat_axis=1, tiled=True)]
    pallas_call x0 -> x3, Pallas kernels: none -> 4.96 us  [the longest x1 2.5 us: project_three(): pl.pallas_call(functools.partial(project_three_kernel, chunks), out_shape...]
    all_to_all x1 -> x0, starting transfers between devices: 4.26 us -> none  [on_device(): lax.all_to_all(inner, 'col', split_axis=2, concat_axis=1, tiled=True)]
  transfers between devices with their start and end apart: 3 -> 0, of which waited for: 2 -> 0; matrix products, arithmetic and copies ran while one was open for 0% -> 0% of each run, Pallas kernels for 0% -> 0%
where the time goes in v1:
time: 67.2 us; the launch traced here: 66.9 us
  blocking collectives  57.4 us (85%)
  Pallas kernels  4.96 us (7%)
  local copies, waits for them, and re-layouts  3.81 us (6%)
  other arithmetic  0.7 us (1%)
    all_to_all x1, blocking collectives, on_device(): lax.all_to_all(shares, 'row', split_axis=0, concat_axis=0, tiled=True)  20.1 us
    all_to_all x1, blocking collectives, on_device(): lax.all_to_all(pieces, 'col', split_axis=0, concat_axis=0, tiled=True)  19.2 us
    all_to_all x1, blocking collectives, on_device(): lax.all_to_all(parts, ('row', 'col'), split_axis=0, concat_axis=0, tiled=...  18.1 us
    unnamed x6, local copies, waits for them, and re-layouts  3.81 us
    pallas_call x1, Pallas kernels, project_three(): pl.pallas_call(functools.partial(project_three_kernel, chunks), out_shape...  2.5 us
    pallas_call x1, Pallas kernels, partial_gram(): pl.pallas_call(functools.partial(gram_kernel, cols), out_shape=jax.ShapeD...  1.79 us

profile of v1, /device:TPU:0, one launch (start us, length us, event | category | flops | bytes accessed | tf_op | source)
XLA Modules:
  0.0 66.9 jit_solution(3498340982197323187)
XLA Ops:
  0.0 0.0 copy-start
  0.0 2.2 %copy-done = bf16[64,64,512]{2,1,0:T(8,128)(2,1)S(1)} copy-done((bf16[64,64,512]{2,1,0:T(8,128)(2,1)S(1)}, bf16[64,64,512]{2,1,0:T(8,128)(2,1)}, u32[]{:S(2)}) %copy-start) | copy-done | bytes 4194328
  2.2 0.0 copy-start.1
  2.2 0.9 %copy-done.1 = bf16[512,128]{1,0:T(8,128)(2,1)S(1)} copy-done((bf16[512,128]{1,0:T(8,128)(2,1)S(1)}, bf16[512,128]{1,0:T(8,128)(2,1)}, u32[]{:S(2)}) %copy-start.1) | copy-done | bytes 131096
  3.1 0.0 copy-start.2
  3.1 0.7 %copy-done.2 = bf16[64,128]{1,0:T(8,128)(2,1)S(1)} copy-done((bf16[64,128]{1,0:T(8,128)(2,1)S(1)}, bf16[64,128]{1,0:T(8,128)(2,1)}, u32[]{:S(2)}) %copy-start.2) | copy-done | bytes 16408
  3.8 2.5 %project_three.1 = bf16[4,1088,128]{2,1,0:T(8,128)(2,1)S(1)} custom-call(bf16[4,16,64,512]{3,2,1,0:T(8,128)(2,1)S(1)} %bitcast.1, bf16[512,128]{1,0:T(8,128)(2,1)S(1)} %copy-done.1, bf16[64,128]{1,0:T(8,128)(2,1)S(1)} %copy-done.2), custom_call_target="tpu_custom_call" | custom-call | tf_op jit(solution)/shard_map/project_three/pallas_call | solution.py:78
  6.3 19.2 %all_to_all.15.recv = bf16[4,1088,128]{2,1,0:T(8,128)(2,1)S(1)} all-to-all(bf16[4,1088,128]{2,1,0:T(8,128)(2,1)S(1)} %project_three.1), channel_id=1, replica_groups=mesh['row'=8,'col'=4] {'col'}, dimensions={0} | all-to-all | bytes 2228224 | tf_op jit(solution)/shard_map/all_to_all | solution.py:192
  25.5 0.7 project_two.1
  26.2 20.1 %all_to_all.16.recv = bf16[8,256,128]{2,1,0:T(8,128)(2,1)S(1)} all-to-all(bf16[8,256,128]{2,1,0:T(8,128)(2,1)S(1)} %project_two.1), channel_id=1, replica_groups=mesh['row'=8,'col'=4] {'row'}, dimensions={0} | all-to-all | bytes 1048576 | tf_op jit(solution)/shard_map/all_to_all | solution.py:194
  46.3 1.8 %partial_gram.1 = bf16[32,64,128]{2,1,0:T(8,128)(2,1)S(1)} custom-call(bf16[8,256,128]{2,1,0:T(8,128)(2,1)S(1)} %all_to_all.16.recv), custom_call_target="tpu_custom_call" | custom-call | tf_op jit(solution)/shard_map/partial_gram/pallas_call | solution.py:176
  48.1 18.1 %all_to_all.17 = bf16[32,64,128]{2,1,0:T(8,128)(2,1)S(1)} all-to-all(bf16[32,64,128]{2,1,0:T(8,128)(2,1)S(1)} %partial_gram.1), channel_id=1, replica_groups=mesh['row'=8,'col'=4] {'row','col'}, dimensions={0} | all-to-all | bytes 1048576 | tf_op jit(solution)/shard_map/all_to_all | solution.py:196
  66.2 0.1 convert_reduce_fusion
  66.3 0.6 broadcast_multiply_fusion
Async XLA Ops:
  0.0 2.2 %copy-start = (bf16[64,64,512]{2,1,0:T(8,128)(2,1)S(1)}, bf16[64,64,512]{2,1,0:T(8,128)(2,1)}, u32[]{:S(2)}) copy-start(bf16[64,64,512]{2,1,0:T(8,128)(2,1)} %param.3) | copy-start | bytes 12582916
  2.2 0.9 %copy-start.1 = (bf16[512,128]{1,0:T(8,128)(2,1)S(1)}, bf16[512,128]{1,0:T(8,128)(2,1)}, u32[]{:S(2)}) copy-start(bf16[512,128]{1,0:T(8,128)(2,1)} %three.1) | copy-start | bytes 393220
  3.1 0.7 %copy-start.2 = (bf16[64,128]{1,0:T(8,128)(2,1)S(1)}, bf16[64,128]{1,0:T(8,128)(2,1)}, u32[]{:S(2)}) copy-start(bf16[64,128]{1,0:T(8,128)(2,1)} %two.1) | copy-start | bytes 49156
